TPU v7x, 32 devices: a whole 2x2x4 slice. The times are simulated.
32 devices in a mesh: row: 8 (over z, x), col: 4 (over y, core).
Axes of the slice: x: 2, y: 2, z: 4, core: 2. Of those that a mesh axis runs over, the one named last changes fastest.
Arguments:
- spikes: int32 [10, 4096], P(None, ('row', 'col')), may hold values 0 or 1
- stp_init: float32 [2, 4096], P(None, ('row', 'col')), may hold values from 0.2 to 1
- trace_init: float32 [3, 4096], P(None, ('row', 'col')), may hold values from 0 to 1.5
- weights: float32 [8, 4, 256, 128, 128], P('row', 'col'), may hold values from 0 to 1
- block_pre: int32 [8, 4, 256], P('row', 'col'), may hold values from 0 to 7
- block_post: int32 [8, 4, 256], P('row', 'col'), may hold values from 0 to 3
- block_count: int32 [8, 4], P('row', 'col'), may hold values from 1 to 255, as said below
Outputs:
- new_weights: float32 [8, 4, 128, 128, 128], P('row', 'col')
- synaptic: float32 [10, 4096], P(None, ('row', 'col'))
Inputs may be any that keep to these rules, and one draw needn't show every extreme that they name: block_count[r, c] + block_count[(r + 4) mod 8, c] = 256; some device uses 2 * 128 - 1 slots in every draw.
All inputs are finite; a program needn't handle non-finite values. No bound on the sum of `spikes` on one device may be relied on, other than what follows from the above.
Results may differ from a plain program's by a relative error of at most 0.0003.
Values sent between devices are 32-bit elements; how exact they have to be, the bound alone decides.
No kernel may reach another device: no remote copies, remote signals or barrier semaphores. Data moves between devices by JAX's collectives and lax.ppermute only.
A program may use at most 128 MiB of HBM per device.

v0:
```python
import math

import jax
import jax.numpy as jnp
from jax import lax
from jax.experimental import pallas as pl
from jax.experimental.pallas import tpu as pltpu
from jax.sharding import PartitionSpec as P


BASE_USE = 0.25
USE_DECAY = 0.98
SUPPLY_RATE = 0.005
PLUS_DECAY = math.exp(-1.0 / 16.8)
MINUS_DECAY = math.exp(-1.0 / 33.7)
SLOW_DECAY = math.exp(-1.0 / 114.0)
SYN_DECAY = math.exp(-1.0 / 5.0)
PAIR_UP = 1.0
TRIPLET_UP = 0.8
PAIR_DOWN = 0.9
LEARN_RATE = 0.02
WEIGHT_MAX = 1.0
INHIB_GAIN = 4.0

CHUNK = 8
UNROLL = 4
FEW = 2
LEAD = 8
LAST = 16


def traces_kernel(spikes, stp_init, trace_init, pre_rows, post_rows):
    steps = spikes.shape[0]
    use_level, supply = stp_init[0:1], stp_init[1:2]
    pre_fast, post_fast, post_slow = trace_init[0:1], trace_init[1:2], trace_init[2:3]
    for t in range(steps):
        s = spikes[t:t + 1].astype(jnp.float32)
        use_level = BASE_USE + (use_level - BASE_USE) * USE_DECAY
        use_level = use_level + s * BASE_USE * (1.0 - use_level)
        release = s * use_level * supply
        supply = supply + SUPPLY_RATE * (1.0 - supply) - release
        pre_fast = pre_fast * PLUS_DECAY + s
        pre_rows[0, t:t + 1] = pre_fast
        pre_rows[0, steps + t:steps + t + 1] = release
        post_rows[0, t:t + 1] = LEARN_RATE * (s * (PAIR_UP + TRIPLET_UP * post_slow))
        post_rows[0, steps + t:steps + t + 1] = -LEARN_RATE * (PAIR_DOWN * post_fast)
        post_fast = post_fast * MINUS_DECAY + s
        post_slow = post_slow * SLOW_DECAY + s


def neuron_traces(spikes, stp_init, trace_init):
    steps, group = spikes.shape
    rows = jax.ShapeDtypeStruct((1, 2 * steps, group), jnp.float32)
    return pl.pallas_call(traces_kernel, out_shape=(rows, rows), name="traces")(
        spikes, stp_init, trace_init
    )


def split(x):
    high = x.astype(jnp.bfloat16).astype(jnp.float32)
    return high, x - high


def updated(block, post, pre):
    change = jnp.dot(post, pre, preferred_element_type=jnp.float32)
    return jnp.clip(block + change, 0.0, WEIGHT_MAX)


def own_kernel(steps, rows, cols, n_pieces):
    stride = -(-2 * steps // 8) * 8
    lo_row = -(-steps // 8) * 8

    def kernel(*refs):
        info, pre_ids, post_ids = refs[:3]
        pieces = refs[3:3 + n_pieces]
        posts, far_posts, weights = refs[3 + n_pieces:6 + n_pieces]
        out, current, pre_out, far_out = refs[6 + n_pieces:10 + n_pieces]
        buf, work, raw_pre, rel, post_t, acc, in_sem, out_sem = refs[10 + n_pieces:]
        group = buf.shape[-1]
        half_chunks = out.shape[0] // CHUNK
        filled, row, col = info[0], info[1], info[2]
        chunks = (filled + CHUNK - 1) // CHUNK
        kept = jnp.minimum(chunks, half_chunks)

        def fetch(i):
            at = pl.ds(i * CHUNK, CHUNK)
            return pltpu.make_async_copy(weights.at[at], buf.at[at], in_sem.at[i])

        def store(i):
            at = pl.ds(i * CHUNK, CHUNK)
            return pltpu.make_async_copy(buf.at[at], out.at[at], out_sem.at[i])

        @pl.loop(0, chunks)
        def _(i):
            fetch(i).start()

        at = 0
        for piece in pieces:
            for k in range(piece.shape[0]):
                raw_pre[at] = piece[k]
                at += 1
        work[...] = jnp.zeros_like(work)

        def spread(value, second, third):
            high, low = split(value)
            pick = (high, low)
            work[0:2 * steps] = high
            work[stride:stride + 2 * steps] = pick[second]
            work[2 * stride:2 * stride + 2 * steps] = pick[third]

        @pl.loop(0, rows)
        def _(k):
            spread(raw_pre[k], 1, 0)
            pre_out[k] = work[...].astype(jnp.bfloat16)

        @pl.loop(0, cols)
        def _(k):
            spread(posts[k], 0, 1)
            post_t[k] = work[...].T.astype(jnp.bfloat16)
            spread(far_posts[k], 0, 1)
            far_out[k] = work[...].T.astype(jnp.bfloat16)

        work[...] = jnp.zeros_like(work)
        lane = lax.broadcasted_iota(jnp.int32, (steps, group), 1)
        polarity = jnp.where(lane % 5 == 4, -INHIB_GAIN, 1.0).astype(jnp.float32)

        @pl.loop(0, rows)
        def _(k):
            high, low = split(raw_pre[k, steps:2 * steps] * polarity)
            work[0:steps] = high
            work[lo_row:lo_row + steps] = low
            turned = work[...].T.astype(jnp.bfloat16)
            rel[k, 0:group] = turned
            rel[k, group:2 * group] = turned

        acc[...] = jnp.zeros_like(acc)

        def slot(s):
            block = buf[s]
            p = pre_ids[s] ^ row
            q = post_ids[s] ^ col
            high = block.astype(jnp.bfloat16)
            low = (block - high.astype(jnp.float32)).astype(jnp.bfloat16)
            both = jnp.concatenate([high, low], axis=1)
            flow = jnp.dot(both, rel[p], preferred_element_type=jnp.float32)
            bin_at = jnp.where(s < filled, q, cols)
            acc[bin_at] = acc[bin_at] + flow
            buf[s] = updated(block, post_t[q], pre_out[p])

        @pl.loop(0, chunks)
        def _(i):
            fetch(i).wait()

            @pl.loop(i * CHUNK, (i + 1) * CHUNK, step=UNROLL)
            def _(s):
                for n in range(UNROLL):
                    slot(s + n)

            @pl.when(i < kept)
            def _():
                store(i).start()

        @pl.loop(0, cols)
        def _(j):
            work[...] = acc[j].T
            current[j] = work[0:steps] + work[lo_row:lo_row + steps]

        @pl.loop(0, kept)
        def _(i):
            store(i).wait()

    return kernel


def own_work(info, pre_ids, post_ids, pieces, posts, far_posts, weights):
    slots, group = weights.shape[0], weights.shape[-1]
    half = slots // 2
    cols, steps = posts.shape[0], posts.shape[1] // 2
    rows = sum(piece.shape[0] for piece in pieces)
    smem = pl.BlockSpec(memory_space=pltpu.SMEM)
    vmem = pl.BlockSpec(memory_space=pltpu.VMEM)
    hbm = pl.BlockSpec(memory_space=pl.ANY)
    square = (group, group)
    return pl.pallas_call(
        own_kernel(steps, rows, cols, len(pieces)),
        out_shape=(
            jax.ShapeDtypeStruct((half,) + square, jnp.float32),
            jax.ShapeDtypeStruct((cols, steps, group), jnp.float32),
            jax.ShapeDtypeStruct((rows,) + square, jnp.bfloat16),
            jax.ShapeDtypeStruct((cols,) + square, jnp.bfloat16),
        ),
        in_specs=[smem] * 3 + [vmem] * (len(pieces) + 2) + [hbm],
        out_specs=(hbm, vmem, vmem, vmem),
        scratch_shapes=[
            pltpu.VMEM((slots,) + square, jnp.float32),
            pltpu.VMEM(square, jnp.float32),
            pltpu.VMEM((rows, 2 * steps, group), jnp.float32),
            pltpu.VMEM((rows, 2 * group, group), jnp.bfloat16),
            pltpu.VMEM((cols,) + square, jnp.bfloat16),
            pltpu.VMEM((cols + 1,) + square, jnp.float32),
            pltpu.SemaphoreType.DMA((slots // CHUNK,)),
            pltpu.SemaphoreType.DMA((half // CHUNK,)),
        ],
        cost_estimate=pl.CostEstimate(flops=10**9, bytes_accessed=2 * 10**7, transcendentals=0),
        name="own_slots",
    )(info, pre_ids, post_ids, *pieces, posts, far_posts, weights)


def received_kernel(first):
    def kernel(info, ids, pre_table, post_table, blocks, _, out, buf, in_sem, out_sem, tail_sem):
        place, row, col, moved = info[0], info[1], info[2], info[3]
        size = blocks.shape[0]
        count = jnp.clip(moved - first, 0, size)
        chunks = (count + CHUNK - 1) // CHUNK
        whole = count // CHUNK

        def fetch(i):
            at = pl.ds(i * CHUNK, CHUNK)
            return pltpu.make_async_copy(blocks.at[at], buf.at[at], in_sem.at[i])

        def store(i):
            at = pl.ds(i * CHUNK, CHUNK)
            to = pl.ds(place + first + i * CHUNK, CHUNK)
            return pltpu.make_async_copy(buf.at[at], out.at[to], out_sem.at[i])

        def store_one(j):
            to = out.at[place + first + j]
            return pltpu.make_async_copy(buf.at[j], to, tail_sem.at[j - whole * CHUNK])

        @pl.loop(0, chunks)
        def _(i):
            fetch(i).start()

        @pl.loop(0, chunks)
        def _(i):
            fetch(i).wait()

            @pl.loop(i * CHUNK, (i + 1) * CHUNK, step=FEW)
            def _(s):
                for n in range(FEW):
                    j = s + n
                    p = ids[0, first + j] ^ row
                    q = ids[1, first + j] ^ col
                    buf[j] = updated(buf[j], post_table[q], pre_table[p])

            @pl.when(i < whole)
            def _():
                store(i).start()

        @pl.loop(whole * CHUNK, count)
        def _(j):
            store_one(j).start()

        @pl.loop(0, whole)
        def _(i):
            store(i).wait()

        @pl.loop(whole * CHUNK, count)
        def _(j):
            store_one(j).wait()

    return kernel


def received_work(first, info, ids, pre_table, post_table, blocks, out):
    smem = pl.BlockSpec(memory_space=pltpu.SMEM)
    vmem = pl.BlockSpec(memory_space=pltpu.VMEM)
    hbm = pl.BlockSpec(memory_space=pl.ANY)
    size = blocks.shape[0]
    return pl.pallas_call(
        received_kernel(first),
        out_shape=jax.ShapeDtypeStruct(out.shape, out.dtype),
        in_specs=[smem, smem, vmem, vmem, hbm, hbm],
        out_specs=hbm,
        scratch_shapes=[
            pltpu.VMEM(blocks.shape, jnp.float32),
            pltpu.SemaphoreType.DMA((size // CHUNK,)),
            pltpu.SemaphoreType.DMA((size // CHUNK,)),
            pltpu.SemaphoreType.DMA((CHUNK,)),
        ],
        input_output_aliases={5: 0},
        cost_estimate=pl.CostEstimate(
            flops=2 * 10**6 * size, bytes_accessed=2**17 * size, transcendentals=0
        ),
        name="received_slots",
    )(info, ids, pre_table, post_table, blocks, out)


def swap(value, axis, mask):
    return lax.ppermute(value, axis, [(n, n ^ mask) for n in range(lax.axis_size(axis))])


def body(spikes, stp_init, trace_init, weights, block_pre, block_post, block_count):
    group = weights.shape[-1]
    half = weights.shape[2] // 2
    steps = spikes.shape[0]
    rows = lax.axis_size("row")
    cols = lax.axis_size("col")
    far = rows // 2
    row = lax.axis_index("row").astype(jnp.int32)
    col = lax.axis_index("col").astype(jnp.int32)
    own_blocks = weights[0, 0]
    pre_ids = block_pre[0, 0]
    post_ids = block_post[0, 0]
    filled = block_count[0, 0]

    far_ids = swap(jnp.stack([pre_ids[half:], post_ids[half:]]), "row", far)
    pre_rows, post_rows = neuron_traces(spikes, stp_init, trace_init)
    posts = jnp.concatenate([post_rows] + [swap(post_rows, "col", m) for m in range(1, cols)])
    near = jnp.concatenate([pre_rows, swap(pre_rows, "row", 1)])
    pieces = [near]
    for m in range(2, rows, 2):
        if m == far:
            got = swap(jnp.concatenate([near, posts]), "row", m)
            pieces.append(got[:2])
            far_posts = got[2:]
        else:
            pieces.append(swap(near, "row", m))

    moved = jnp.abs(filled - half)
    sending = filled > half
    upward = sending == (row < far)
    info = jnp.stack([filled, row, col, jnp.where(sending, 0, moved)])
    quarter = half // 4
    sizes = list(range(CHUNK, quarter, CHUNK)) + list(range(quarter, half + 1, 2 * CHUNK))
    sizes = sizes[::-1]
    kind = sum((moved <= size).astype(jnp.int32) for size in sizes)
    choice = jnp.where(moved == 0, 2 * len(sizes), 2 * (kind - 1) + upward.astype(jnp.int32))
    up_pairs = [(n, n + far) for n in range(far)]
    down_pairs = [(n + far, n) for n in range(far)]

    def branch(size, pairs):
        def run(info, pre_ids, post_ids, far_ids, posts, far_posts, blocks, *pieces):
            if size > half // 2 + LAST:
                cuts = [0, LEAD, size - LAST, size]
            elif size > quarter:
                cuts = [0, LEAD, size]
            else:
                cuts = [0, size][:size + 1]
            parts = []
            for a, b in zip(cuts[:-1], cuts[1:]):
                part = blocks[half + a:half + b]
                parts.append((a, lax.ppermute(part, "row", pairs)))
            out, current, pre_table, far_table = own_work(
                info, pre_ids, post_ids, pieces, posts, far_posts, blocks
            )
            for a, part in parts:
                out = received_work(a, info, far_ids, pre_table, far_table, part, out)
            return out, current

        return run

    branches = []
    for size in sizes:
        branches += [branch(size, down_pairs), branch(size, up_pairs)]
    branches.append(branch(0, up_pairs))
    new_blocks, current = lax.switch(
        choice, branches,
        info, pre_ids, post_ids, far_ids, posts, far_posts, own_blocks, *pieces,
    )
    drive = current[0]
    for m in range(1, cols):
        drive = drive + swap(current[m], "col", m)
    gain = 1.0 / math.sqrt(group * half)
    state = jnp.zeros_like(drive[0])
    filtered = []
    for step in range(steps):
        state = state * SYN_DECAY + gain * drive[step]
        filtered.append(state)
    return (new_blocks[None, None], jnp.stack(filtered))


def solution(mesh):
    placed = (
        P(None, ("row", "col")),
        P(None, ("row", "col")),
        P(None, ("row", "col")),
        P("row", "col", None, None, None),
        P("row", "col", None),
        P("row", "col", None),
        P("row", "col"),
    )
    return jax.shard_map(
        body,
        mesh=mesh,
        in_specs=placed,
        out_specs=(P("row", "col", None, None, None), P(None, ("row", "col"))),
        check_vma=False,
    )
```

profile of v0, /device:TPU:25, one launch (start us, length us, event | category | flops | bytes accessed | tf_op | source)
XLA Modules:
  0.0 227.6 jit_solution(9518445971725197477)
XLA Ops:
  0.6 1.4 traces.1
  2.0 0.7 collective-permute-start.40
  2.7 1.2 collective-permute-start.41
  3.9 0.4 collective-permute-start.42
  4.3 1.2 collective-permute-start.38
  5.5 0.7 slice_bitcast_fusion.3
  6.2 0.1 collective-permute-start.45
  6.3 0.7 constant_dynamic-update-slice_fusion.7
  7.7 0.0 collective-permute-done.38
  7.7 0.7 constant_dynamic-update-slice_fusion.11
  8.4 0.2 collective-permute-start.39
  8.6 0.0 collective-permute-done.40
  8.6 3.3 %collective-permute-start.44 = (f32[2,20,128]{2,1,0:T(8,128)S(1)}, f32[2,20,128]{2,1,0:T(8,128)S(1)}, u32[]{:S(2)}, u32[]{:S(2)}) collective-permute-start(f32[2,20,128]{2,1,0:T(8,128)S(1)} %get-tuple-element.804), channel_id=1, source_target_pairs={{0,24},{4,28},{8,16},{12,20},{16,8},{20,12},{24,0},{28,4},{1,25},{... | collective-permute-start | bytes 61448 | tf_op jit(solution)/shard_map/ppermute | solution.py:290
  11.9 0.0 collective-permute-done.41
  11.9 0.0 collective-permute-done.42
  12.0 0.1 collective-permute-start.43
  12.1 0.1 pad_add_fusion.1
  12.1 4.1 %collective-permute-done.43 = f32[6,20,128]{2,1,0:T(8,128)S(1)} collective-permute-done((f32[6,20,128]{2,1,0:T(8,128)S(1)}, f32[6,20,128]{2,1,0:T(8,128)S(1)}, u32[]{:S(2)}, u32[]{:S(2)}) %collective-permute-start.43) | collective-permute-done | bytes 61472 | tf_op jit(solution)/shard_map/ppermute | solution.py:290
  16.3 0.0 collective-permute-done.39
  16.3 0.0 collective-permute-done.44
  16.3 0.0 collective-permute-done.45
  16.3 71.7 %conditional.1 = (f32[4,10,128]{2,1,0:T(8,128)S(1)}, f32[1,1,128,128,128]{4,3,2,1,0:T(8,128)}) conditional(s32[]{:T(128)} %clamp.3, (s32[4]{0:T(128)S(1)}, s32[256]{0:T(256)}, s32[256]{0:T(256)}, f32[2,20,128]{2,1,0:T(8,128)S(1)}, f32[2,20,128]{2,1,0:T(8,128)S(1)}, /*index=5*/f32[2,20,128]{2,1,0:T(8,128)S(1)}, ...), branch_computations={%region_0.1_spmd, %region_1.2_spmd, %region_2.3_spmd, %region_3.4_... | conditional | flops 1256000000 | bytes 93408760 | solution.py:357
  16.6 1.9 slice.142
  18.5 1.3 collective-permute-start.28
  19.8 1.1 slice.143
  20.9 1.3 collective-permute-start.29
  22.2 10.8 %own_slots.32 = (f32[128,128,128]{2,1,0:T(8,128)}, f32[4,10,128]{2,1,0:T(8,128)S(1)}, bf16[8,128,128]{2,1,0:T(8,128)(2,1)}, bf16[4,128,128]{2,1,0:T(8,128)(2,1)}) custom-call(s32[4]{0:T(128)S(1)} %get-tuple-element.626.refs_0_.info, s32[256]{0:T(256)} %get-tuple-element.627.refs_1_, s32[256]{0:T(256)} %get-tuple-element.628.refs_2_, ...), custom_call_target="tpu_custom_call" | custom-call | flops 1000000000 | bytes 20000000 | tf_op jit(solution)/shard_map/cond/branch_11_fun/own_slots/pallas_call | solution.py:184
  32.9 46.1 %collective-permute-done.29.blocks = f32[8,128,128]{2,1,0:T(8,128)} collective-permute-done((f32[8,128,128]{2,1,0:T(8,128)S(1)}, f32[8,128,128]{2,1,0:T(8,128)}, u32[]{:S(2)}, u32[]{:S(2)}) %collective-permute-start.29) | collective-permute-done | bytes 524320 | tf_op jit(solution)/shard_map/cond/branch_11_fun/ppermute | solution.py:343
  79.0 3.6 %received_slots.66._ = f32[128,128,128]{2,1,0:T(8,128)} custom-call(s32[4]{0:T(128)S(1)} %get-tuple-element.626.refs_0_.info, s32[2,128]{1,0:T(2,128)S(1)} %get-tuple-element.637.ids, bf16[8,128,128]{2,1,0:T(8,128)(2,1)} %get-tuple-element.638.pre_table, bf16[4,128,128]{2,1,0:T(8,128)(2,1)} %get-tuple-element.639.post_table, ...), custom_call_target="tpu_custom_call", output_to_operand_aliasing={{}: (5, {})} | custom-call | flops 16000000 | bytes 1048576 | tf_op jit(solution)/shard_map/cond/branch_11_fun/received_slots/pallas_call | solution.py:270
  82.6 0.0 collective-permute-done.28.blocks
  82.6 5.4 %received_slots.67 = f32[128,128,128]{2,1,0:T(8,128)} custom-call(s32[4]{0:T(128)S(1)} %get-tuple-element.626.refs_0_.info, s32[2,128]{1,0:T(2,128)S(1)} %get-tuple-element.637.ids, bf16[8,128,128]{2,1,0:T(8,128)(2,1)} %get-tuple-element.638.pre_table, bf16[4,128,128]{2,1,0:T(8,128)(2,1)} %get-tuple-element.639.post_table, ...), custom_call_target="tpu_custom_call", output_to_operand_aliasing={{}: (5, {})} | custom-call | flops 80000000 | bytes 5242880 | tf_op jit(solution)/shard_map/cond/branch_11_fun/received_slots/pallas_call | solution.py:270
  88.0 0.1 collective-permute-start.46
  88.1 134.8 %collective-permute-start.47 = (f32[10,128]{1,0:T(8,128)S(1)}, f32[10,128]{1,0:T(8,128)S(1)}, u32[]{:S(2)}, u32[]{:S(2)}) collective-permute-start(f32[10,128]{1,0:T(8,128)S(1)} %get-tuple-element.794), channel_id=1, source_target_pairs={{0,2},{1,3},{2,0},{3,1},{4,6},{5,7},{6,4},{7,5},{8,10},{9,11},{10,... | collective-permute-start | bytes 15368 | tf_op jit(solution)/shard_map/ppermute | solution.py:290
  222.9 0.3 collective-permute-start.48
  223.3 0.0 collective-permute-done.46
  223.3 0.7 collective-permute-done.47
  224.0 2.4 %collective-permute-done.48 = f32[10,128]{1,0:T(8,128)S(1)} collective-permute-done((f32[10,128]{1,0:T(8,128)S(1)}, f32[10,128]{1,0:T(8,128)S(1)}, u32[]{:S(2)}, u32[]{:S(2)}) %collective-permute-start.48) | collective-permute-done | bytes 5152 | tf_op jit(solution)/shard_map/ppermute | solution.py:290
  226.4 1.2 stack.41
  (10 shorter events, 0.1 us)
Async XLA Ops:
  2.0 6.6 %collective-permute-start.40 = (f32[1,20,128]{2,1,0:T(8,128)}, f32[1,20,128]{2,1,0:T(8,128)S(1)}, u32[]{:S(2)}, u32[]{:S(2)}) collective-permute-start(f32[1,20,128]{2,1,0:T(8,128)} %get-tuple-element.780), channel_id=1, source_target_pairs={{0,1},{1,0},{2,3},{3,2},{4,5},{5,4},{6,7},{7,6},{8,9},{9,8},{10,11... | collective-permute-start | bytes 30728 | tf_op jit(solution)/shard_map/ppermute | solution.py:290
  2.7 9.3 %collective-permute-start.41 = (f32[1,20,128]{2,1,0:T(8,128)}, f32[1,20,128]{2,1,0:T(8,128)S(1)}, u32[]{:S(2)}, u32[]{:S(2)}) collective-permute-start(f32[1,20,128]{2,1,0:T(8,128)} %get-tuple-element.780), channel_id=1, source_target_pairs={{0,2},{1,3},{2,0},{3,1},{4,6},{5,7},{6,4},{7,5},{8,10},{9,11},{10,... | collective-permute-start | bytes 30728 | tf_op jit(solution)/shard_map/ppermute | solution.py:290
  3.9 8.0 %collective-permute-start.42 = (f32[1,20,128]{2,1,0:T(8,128)}, f32[1,20,128]{2,1,0:T(8,128)S(1)}, u32[]{:S(2)}, u32[]{:S(2)}) collective-permute-start(f32[1,20,128]{2,1,0:T(8,128)} %get-tuple-element.780), channel_id=1, source_target_pairs={{0,3},{1,2},{2,1},{3,0},{4,7},{5,6},{6,5},{7,4},{8,11},{9,10},{10,... | collective-permute-start | bytes 30728 | tf_op jit(solution)/shard_map/ppermute | solution.py:290
  4.3 3.4 %collective-permute-start.38 = (f32[1,20,128]{2,1,0:T(8,128)}, f32[1,20,128]{2,1,0:T(8,128)S(1)}, u32[]{:S(2)}, u32[]{:S(2)}) collective-permute-start(f32[1,20,128]{2,1,0:T(8,128)} %get-tuple-element.779), channel_id=1, source_target_pairs={{0,4},{4,0},{8,12},{12,8},{16,20},{20,16},{24,28},{28,24},{1,5},{5... | collective-permute-start | bytes 30728 | tf_op jit(solution)/shard_map/ppermute | solution.py:290
  6.2 10.1 %collective-permute-start.45 = (s32[2,128]{1,0:T(2,128)S(1)}, s32[2,128]{1,0:T(2,128)S(1)}, u32[]{:S(2)}, u32[]{:S(2)}) collective-permute-start(s32[2,128]{1,0:T(2,128)S(1)} %pad_add_fusion), channel_id=1, source_target_pairs={{0,16},{4,20},{8,24},{12,28},{16,0},{20,4},{24,8},{28,12},{1,17},{... | collective-permute-start | bytes 3080 | tf_op jit(solution)/shard_map/ppermute | solution.py:290
  8.4 7.8 %collective-permute-start.39 = (f32[2,20,128]{2,1,0:T(8,128)S(1)}, f32[2,20,128]{2,1,0:T(8,128)S(1)}, u32[]{:S(2)}, u32[]{:S(2)}) collective-permute-start(f32[2,20,128]{2,1,0:T(8,128)S(1)} %get-tuple-element.804), channel_id=1, source_target_pairs={{0,8},{4,12},{8,0},{12,4},{16,24},{20,28},{24,16},{28,20},{1,9},{5... | collective-permute-start | bytes 61448 | tf_op jit(solution)/shard_map/ppermute | solution.py:290
  8.6 7.7 %collective-permute-start.44 = (f32[2,20,128]{2,1,0:T(8,128)S(1)}, f32[2,20,128]{2,1,0:T(8,128)S(1)}, u32[]{:S(2)}, u32[]{:S(2)}) collective-permute-start(f32[2,20,128]{2,1,0:T(8,128)S(1)} %get-tuple-element.804), channel_id=1, source_target_pairs={{0,24},{4,28},{8,16},{12,20},{16,8},{20,12},{24,0},{28,4},{1,25},{... | collective-permute-start | bytes 61448 | tf_op jit(solution)/shard_map/ppermute | solution.py:290
  12.0 4.3 %collective-permute-start.43 = (f32[6,20,128]{2,1,0:T(8,128)S(1)}, f32[6,20,128]{2,1,0:T(8,128)S(1)}, u32[]{:S(2)}, u32[]{:S(2)}) collective-permute-start(f32[6,20,128]{2,1,0:T(8,128)S(1)} %get-tuple-element.796), channel_id=1, source_target_pairs={{0,16},{4,20},{8,24},{12,28},{16,0},{20,4},{24,8},{28,12},{1,17},{... | collective-permute-start | bytes 184328 | tf_op jit(solution)/shard_map/ppermute | solution.py:290
  18.5 64.1 %collective-permute-start.28 = (f32[40,128,128]{2,1,0:T(8,128)S(1)}, f32[40,128,128]{2,1,0:T(8,128)}, u32[]{:S(2)}, u32[]{:S(2)}) collective-permute-start(f32[40,128,128]{2,1,0:T(8,128)S(1)} %slice.142), channel_id=1, source_target_pairs={{0,16},{4,20},{8,24},{12,28},{1,17},{5,21},{9,25},{13,29},{2,18},{... | collective-permute-start | bytes 7864328 | tf_op jit(solution)/shard_map/cond/branch_11_fun/ppermute | solution.py:343
  20.9 58.1 %collective-permute-start.29 = (f32[8,128,128]{2,1,0:T(8,128)S(1)}, f32[8,128,128]{2,1,0:T(8,128)}, u32[]{:S(2)}, u32[]{:S(2)}) collective-permute-start(f32[8,128,128]{2,1,0:T(8,128)S(1)} %slice.143), channel_id=1, source_target_pairs={{0,16},{4,20},{8,24},{12,28},{1,17},{5,21},{9,25},{13,29},{2,18},{... | collective-permute-start | bytes 1572872 | tf_op jit(solution)/shard_map/cond/branch_11_fun/ppermute | solution.py:343
  88.0 135.2 %collective-permute-start.46 = (f32[10,128]{1,0:T(8,128)S(1)}, f32[10,128]{1,0:T(8,128)S(1)}, u32[]{:S(2)}, u32[]{:S(2)}) collective-permute-start(f32[10,128]{1,0:T(8,128)S(1)} %get-tuple-element.792), channel_id=1, source_target_pairs={{0,1},{1,0},{2,3},{3,2},{4,5},{5,4},{6,7},{7,6},{8,9},{9,8},{10,11... | collective-permute-start | bytes 15368 | tf_op jit(solution)/shard_map/ppermute | solution.py:290
  88.1 135.9 %collective-permute-start.47 = (f32[10,128]{1,0:T(8,128)S(1)}, f32[10,128]{1,0:T(8,128)S(1)}, u32[]{:S(2)}, u32[]{:S(2)}) collective-permute-start(f32[10,128]{1,0:T(8,128)S(1)} %get-tuple-element.794), channel_id=1, source_target_pairs={{0,2},{1,3},{2,0},{3,1},{4,6},{5,7},{6,4},{7,5},{8,10},{9,11},{10,... | collective-permute-start | bytes 15368 | tf_op jit(solution)/shard_map/ppermute | solution.py:290
  222.9 3.4 %collective-permute-start.48 = (f32[10,128]{1,0:T(8,128)S(1)}, f32[10,128]{1,0:T(8,128)S(1)}, u32[]{:S(2)}, u32[]{:S(2)}) collective-permute-start(f32[10,128]{1,0:T(8,128)S(1)} %get-tuple-element.793), channel_id=1, source_target_pairs={{0,3},{1,2},{2,1},{3,0},{4,7},{5,6},{6,5},{7,4},{8,11},{9,10},{10,... | collective-permute-start | bytes 15368 | tf_op jit(solution)/shard_map/ppermute | solution.py:290
where the time goes:
time: 228 us
  starting transfers between devices  145 us (64%)
  waiting for transfers between devices  53.3 us (23%)
  Pallas kernels  21.1 us (9%)
  local copies, waits for them, and re-layouts  6.33 us (3%)
    ppermute x11, starting transfers between devices, swap(): lax.ppermute(value, axis, [(n, n ^ mask) for n in range(lax.axis_size(axi...  142 us
    ppermute x2, waiting for transfers between devices, run(): parts.append((a, lax.ppermute(part, 'row', pairs)))  46.1 us
    pallas_call x1, Pallas kernels, own_work(): pl.pallas_call(own_kernel(steps, rows, cols, len(pieces)), out_shape=(jax...  10.8 us
    pallas_call x2, Pallas kernels, received_work(): pl.pallas_call(received_kernel(first), out_shape=jax.ShapeDtypeStruct(out...  8.97 us
    ppermute x11, waiting for transfers between devices, swap(): lax.ppermute(value, axis, [(n, n ^ mask) for n in range(lax.axis_size(axi...  7.24 us
  transfers between devices with their start and end apart: 13, of which 4 were waited for; matrix products, arithmetic and copies ran while one was open for 1% of the time, Pallas kernels for 6%

commit v1 on v0

--- a/solution.py
+++ b/solution.py
@@ -24,9 +24,9 @@
 
 CHUNK = 8
 UNROLL = 4
-FEW = 2
+FEW = 4
 LEAD = 8
-LAST = 16
+LAST = 8
 
 
 def traces_kernel(spikes, stp_init, trace_init, pre_rows, post_rows):
@@ -331,7 +331,7 @@
 
     def branch(size, pairs):
         def run(info, pre_ids, post_ids, far_ids, posts, far_posts, blocks, *pieces):
-            if size > half // 2 + LAST:
+            if size > half * 5 // 8:
                 cuts = [0, LEAD, size - LAST, size]
             elif size > quarter:
                 cuts = [0, LEAD, size]

time: 228 us -> 218 us (0.956)
  starting transfers between devices: 145 us -> 136 us
    ppermute x11, starting transfers between devices: 142 us -> 134 us  [swap(): lax.ppermute(value, axis, [(n, n ^ mask) for n in range(lax.axis_size(axi...]
  transfers between devices with their start and end apart: 13 -> 13, of which waited for: 4 -> 4; matrix products, arithmetic and copies ran while one was open for 1% -> 2% of each run, Pallas kernels for 6% -> 6%
where the time goes in v1:
time: 218 us
  starting transfers between devices  136 us (62%)
  waiting for transfers between devices  53.3 us (24%)
  Pallas kernels  19.8 us (9%)
  local copies, waits for them, and re-layouts  6.33 us (3%)
    ppermute x11, starting transfers between devices, swap(): lax.ppermute(value, axis, [(n, n ^ mask) for n in range(lax.axis_size(axi...  134 us
    ppermute x2, waiting for transfers between devices, run(): parts.append((a, lax.ppermute(part, 'row', pairs)))  46.1 us
    pallas_call x1, Pallas kernels, own_work(): pl.pallas_call(own_kernel(steps, rows, cols, len(pieces)), out_shape=(jax...  10.8 us
    pallas_call x2, Pallas kernels, received_work(): pl.pallas_call(received_kernel(first), out_shape=jax.ShapeDtypeStruct(out...  7.62 us
    ppermute x11, waiting for transfers between devices, swap(): lax.ppermute(value, axis, [(n, n ^ mask) for n in range(lax.axis_size(axi...  7.24 us
  transfers between devices with their start and end apart: 13, of which 4 were waited for; matrix products, arithmetic and copies ran while one was open for 2% of the time, Pallas kernels for 6%

profile of v1, /device:TPU:25, one launch (start us, length us, event | category | flops | bytes accessed | tf_op | source)
XLA Modules:
  0.0 217.6 jit_solution(2298975716221788269)
XLA Ops:
  0.6 1.4 traces.1
  2.0 0.7 collective-permute-start.40
  2.7 1.2 collective-permute-start.41
  3.9 0.4 collective-permute-start.42
  4.3 1.2 collective-permute-start.38
  5.5 0.7 slice_bitcast_fusion.3
  6.2 0.1 collective-permute-start.45
  6.3 0.7 constant_dynamic-update-slice_fusion.7
  7.7 0.0 collective-permute-done.38
  7.7 0.7 constant_dynamic-update-slice_fusion.11
  8.4 0.2 collective-permute-start.39
  8.6 0.0 collective-permute-done.40
  8.6 3.3 %collective-permute-start.44 = (f32[2,20,128]{2,1,0:T(8,128)S(1)}, f32[2,20,128]{2,1,0:T(8,128)S(1)}, u32[]{:S(2)}, u32[]{:S(2)}) collective-permute-start(f32[2,20,128]{2,1,0:T(8,128)S(1)} %get-tuple-element.816), channel_id=1, source_target_pairs={{0,24},{4,28},{8,16},{12,20},{16,8},{20,12},{24,0},{28,4},{1,25},{... | collective-permute-start | bytes 61448 | tf_op jit(solution)/shard_map/ppermute | solution.py:290
  11.9 0.0 collective-permute-done.41
  11.9 0.0 collective-permute-done.42
  12.0 0.1 collective-permute-start.43
  12.1 0.1 pad_add_fusion.1
  12.1 4.1 %collective-permute-done.43 = f32[6,20,128]{2,1,0:T(8,128)S(1)} collective-permute-done((f32[6,20,128]{2,1,0:T(8,128)S(1)}, f32[6,20,128]{2,1,0:T(8,128)S(1)}, u32[]{:S(2)}, u32[]{:S(2)}) %collective-permute-start.43) | collective-permute-done | bytes 61472 | tf_op jit(solution)/shard_map/ppermute | solution.py:290
  16.3 0.0 collective-permute-done.39
  16.3 0.0 collective-permute-done.44
  16.3 0.0 collective-permute-done.45
  16.3 70.4 %conditional.1 = (f32[4,10,128]{2,1,0:T(8,128)S(1)}, f32[1,1,128,128,128]{4,3,2,1,0:T(8,128)}) conditional(s32[]{:T(128)} %clamp.3, (s32[4]{0:T(128)S(1)}, s32[256]{0:T(256)}, s32[256]{0:T(256)}, f32[2,20,128]{2,1,0:T(8,128)S(1)}, f32[2,20,128]{2,1,0:T(8,128)S(1)}, /*index=5*/f32[2,20,128]{2,1,0:T(8,128)S(1)}, ...), branch_computations={%region_0.1_spmd, %region_1.2_spmd, %region_2.3_spmd, %region_3.4_... | conditional | flops 1256000000 | bytes 91311608 | solution.py:357
  16.6 1.9 slice.142
  18.5 1.3 collective-permute-start.10
  19.8 1.1 slice.143
  20.9 1.3 collective-permute-start.11
  22.2 10.8 %own_slots.32 = (f32[128,128,128]{2,1,0:T(8,128)}, f32[4,10,128]{2,1,0:T(8,128)S(1)}, bf16[8,128,128]{2,1,0:T(8,128)(2,1)}, bf16[4,128,128]{2,1,0:T(8,128)(2,1)}) custom-call(s32[4]{0:T(128)S(1)} %get-tuple-element.626.refs_0_.info, s32[256]{0:T(256)} %get-tuple-element.627.refs_1_, s32[256]{0:T(256)} %get-tuple-element.628.refs_2_, ...), custom_call_target="tpu_custom_call" | custom-call | flops 1000000000 | bytes 20000000 | tf_op jit(solution)/shard_map/cond/branch_11_fun/own_slots/pallas_call | solution.py:184
  32.9 46.1 %collective-permute-done.11.blocks = f32[8,128,128]{2,1,0:T(8,128)} collective-permute-done((f32[8,128,128]{2,1,0:T(8,128)S(1)}, f32[8,128,128]{2,1,0:T(8,128)}, u32[]{:S(2)}, u32[]{:S(2)}) %collective-permute-start.11) | collective-permute-done | bytes 524320 | tf_op jit(solution)/shard_map/cond/branch_11_fun/ppermute | solution.py:343
  79.0 3.3 %received_slots.66._ = f32[128,128,128]{2,1,0:T(8,128)} custom-call(s32[4]{0:T(128)S(1)} %get-tuple-element.626.refs_0_.info, s32[2,128]{1,0:T(2,128)S(1)} %get-tuple-element.637.ids, bf16[8,128,128]{2,1,0:T(8,128)(2,1)} %get-tuple-element.638.pre_table, bf16[4,128,128]{2,1,0:T(8,128)(2,1)} %get-tuple-element.639.post_table, ...), custom_call_target="tpu_custom_call", output_to_operand_aliasing={{}: (5, {})} | custom-call | flops 16000000 | bytes 1048576 | tf_op jit(solution)/shard_map/cond/branch_11_fun/received_slots/pallas_call | solution.py:270
  82.3 0.0 collective-permute-done.10.blocks
  82.3 4.3 %received_slots.67 = f32[128,128,128]{2,1,0:T(8,128)} custom-call(s32[4]{0:T(128)S(1)} %get-tuple-element.626.refs_0_.info, s32[2,128]{1,0:T(2,128)S(1)} %get-tuple-element.637.ids, bf16[8,128,128]{2,1,0:T(8,128)(2,1)} %get-tuple-element.638.pre_table, bf16[4,128,128]{2,1,0:T(8,128)(2,1)} %get-tuple-element.639.post_table, ...), custom_call_target="tpu_custom_call", output_to_operand_aliasing={{}: (5, {})} | custom-call | flops 80000000 | bytes 5242880 | tf_op jit(solution)/shard_map/cond/branch_11_fun/received_slots/pallas_call | solution.py:270
  86.7 0.5 collective-permute-start.46
  87.1 125.7 %collective-permute-start.47 = (f32[10,128]{1,0:T(8,128)S(1)}, f32[10,128]{1,0:T(8,128)S(1)}, u32[]{:S(2)}, u32[]{:S(2)}) collective-permute-start(f32[10,128]{1,0:T(8,128)S(1)} %get-tuple-element.806), channel_id=1, source_target_pairs={{0,2},{1,3},{2,0},{3,1},{4,6},{5,7},{6,4},{7,5},{8,10},{9,11},{10,... | collective-permute-start | bytes 15368 | tf_op jit(solution)/shard_map/ppermute | solution.py:290
  212.9 0.3 collective-permute-start.48
  213.2 0.0 collective-permute-done.46
  213.2 0.7 collective-permute-done.47
  213.9 2.4 %collective-permute-done.48 = f32[10,128]{1,0:T(8,128)S(1)} collective-permute-done((f32[10,128]{1,0:T(8,128)S(1)}, f32[10,128]{1,0:T(8,128)S(1)}, u32[]{:S(2)}, u32[]{:S(2)}) %collective-permute-start.48) | collective-permute-done | bytes 5152 | tf_op jit(solution)/shard_map/ppermute | solution.py:290
  216.3 1.2 stack.41
  (10 shorter events, 0.1 us)
Async XLA Ops:
  2.0 6.6 %collective-permute-start.40 = (f32[1,20,128]{2,1,0:T(8,128)}, f32[1,20,128]{2,1,0:T(8,128)S(1)}, u32[]{:S(2)}, u32[]{:S(2)}) collective-permute-start(f32[1,20,128]{2,1,0:T(8,128)} %get-tuple-element.780), channel_id=1, source_target_pairs={{0,1},{1,0},{2,3},{3,2},{4,5},{5,4},{6,7},{7,6},{8,9},{9,8},{10,11... | collective-permute-start | bytes 30728 | tf_op jit(solution)/shard_map/ppermute | solution.py:290
  2.7 9.3 %collective-permute-start.41 = (f32[1,20,128]{2,1,0:T(8,128)}, f32[1,20,128]{2,1,0:T(8,128)S(1)}, u32[]{:S(2)}, u32[]{:S(2)}) collective-permute-start(f32[1,20,128]{2,1,0:T(8,128)} %get-tuple-element.780), channel_id=1, source_target_pairs={{0,2},{1,3},{2,0},{3,1},{4,6},{5,7},{6,4},{7,5},{8,10},{9,11},{10,... | collective-permute-start | bytes 30728 | tf_op jit(solution)/shard_map/ppermute | solution.py:290
  3.9 8.0 %collective-permute-start.42 = (f32[1,20,128]{2,1,0:T(8,128)}, f32[1,20,128]{2,1,0:T(8,128)S(1)}, u32[]{:S(2)}, u32[]{:S(2)}) collective-permute-start(f32[1,20,128]{2,1,0:T(8,128)} %get-tuple-element.780), channel_id=1, source_target_pairs={{0,3},{1,2},{2,1},{3,0},{4,7},{5,6},{6,5},{7,4},{8,11},{9,10},{10,... | collective-permute-start | bytes 30728 | tf_op jit(solution)/shard_map/ppermute | solution.py:290
  4.3 3.4 %collective-permute-start.38 = (f32[1,20,128]{2,1,0:T(8,128)}, f32[1,20,128]{2,1,0:T(8,128)S(1)}, u32[]{:S(2)}, u32[]{:S(2)}) collective-permute-start(f32[1,20,128]{2,1,0:T(8,128)} %get-tuple-element.779), channel_id=1, source_target_pairs={{0,4},{4,0},{8,12},{12,8},{16,20},{20,16},{24,28},{28,24},{1,5},{5... | collective-permute-start | bytes 30728 | tf_op jit(solution)/shard_map/ppermute | solution.py:290
  6.2 10.1 %collective-permute-start.45 = (s32[2,128]{1,0:T(2,128)S(1)}, s32[2,128]{1,0:T(2,128)S(1)}, u32[]{:S(2)}, u32[]{:S(2)}) collective-permute-start(s32[2,128]{1,0:T(2,128)S(1)} %pad_add_fusion), channel_id=1, source_target_pairs={{0,16},{4,20},{8,24},{12,28},{16,0},{20,4},{24,8},{28,12},{1,17},{... | collective-permute-start | bytes 3080 | tf_op jit(solution)/shard_map/ppermute | solution.py:290
  8.4 7.8 %collective-permute-start.39 = (f32[2,20,128]{2,1,0:T(8,128)S(1)}, f32[2,20,128]{2,1,0:T(8,128)S(1)}, u32[]{:S(2)}, u32[]{:S(2)}) collective-permute-start(f32[2,20,128]{2,1,0:T(8,128)S(1)} %get-tuple-element.816), channel_id=1, source_target_pairs={{0,8},{4,12},{8,0},{12,4},{16,24},{20,28},{24,16},{28,20},{1,9},{5... | collective-permute-start | bytes 61448 | tf_op jit(solution)/shard_map/ppermute | solution.py:290
  8.6 7.7 %collective-permute-start.44 = (f32[2,20,128]{2,1,0:T(8,128)S(1)}, f32[2,20,128]{2,1,0:T(8,128)S(1)}, u32[]{:S(2)}, u32[]{:S(2)}) collective-permute-start(f32[2,20,128]{2,1,0:T(8,128)S(1)} %get-tuple-element.816), channel_id=1, source_target_pairs={{0,24},{4,28},{8,16},{12,20},{16,8},{20,12},{24,0},{28,4},{1,25},{... | collective-permute-start | bytes 61448 | tf_op jit(solution)/shard_map/ppermute | solution.py:290
  12.0 4.3 %collective-permute-start.43 = (f32[6,20,128]{2,1,0:T(8,128)S(1)}, f32[6,20,128]{2,1,0:T(8,128)S(1)}, u32[]{:S(2)}, u32[]{:S(2)}) collective-permute-start(f32[6,20,128]{2,1,0:T(8,128)S(1)} %get-tuple-element.808), channel_id=1, source_target_pairs={{0,16},{4,20},{8,24},{12,28},{16,0},{20,4},{24,8},{28,12},{1,17},{... | collective-permute-start | bytes 184328 | tf_op jit(solution)/shard_map/ppermute | solution.py:290
  18.5 63.8 %collective-permute-start.10 = (f32[40,128,128]{2,1,0:T(8,128)S(1)}, f32[40,128,128]{2,1,0:T(8,128)}, u32[]{:S(2)}, u32[]{:S(2)}) collective-permute-start(f32[40,128,128]{2,1,0:T(8,128)S(1)} %slice.142), channel_id=1, source_target_pairs={{0,16},{4,20},{8,24},{12,28},{1,17},{5,21},{9,25},{13,29},{2,18},{... | collective-permute-start | bytes 7864328 | tf_op jit(solution)/shard_map/cond/branch_11_fun/ppermute | solution.py:343
  20.9 58.1 %collective-permute-start.11 = (f32[8,128,128]{2,1,0:T(8,128)S(1)}, f32[8,128,128]{2,1,0:T(8,128)}, u32[]{:S(2)}, u32[]{:S(2)}) collective-permute-start(f32[8,128,128]{2,1,0:T(8,128)S(1)} %slice.143), channel_id=1, source_target_pairs={{0,16},{4,20},{8,24},{12,28},{1,17},{5,21},{9,25},{13,29},{2,18},{... | collective-permute-start | bytes 1572872 | tf_op jit(solution)/shard_map/cond/branch_11_fun/ppermute | solution.py:343
  86.7 126.5 %collective-permute-start.46 = (f32[10,128]{1,0:T(8,128)S(1)}, f32[10,128]{1,0:T(8,128)S(1)}, u32[]{:S(2)}, u32[]{:S(2)}) collective-permute-start(f32[10,128]{1,0:T(8,128)S(1)} %get-tuple-element.804), channel_id=1, source_target_pairs={{0,1},{1,0},{2,3},{3,2},{4,5},{5,4},{6,7},{7,6},{8,9},{9,8},{10,11... | collective-permute-start | bytes 15368 | tf_op jit(solution)/shard_map/ppermute | solution.py:290
  87.1 126.8 %collective-permute-start.47 = (f32[10,128]{1,0:T(8,128)S(1)}, f32[10,128]{1,0:T(8,128)S(1)}, u32[]{:S(2)}, u32[]{:S(2)}) collective-permute-start(f32[10,128]{1,0:T(8,128)S(1)} %get-tuple-element.806), channel_id=1, source_target_pairs={{0,2},{1,3},{2,0},{3,1},{4,6},{5,7},{6,4},{7,5},{8,10},{9,11},{10,... | collective-permute-start | bytes 15368 | tf_op jit(solution)/shard_map/ppermute | solution.py:290
  212.9 3.4 %collective-permute-start.48 = (f32[10,128]{1,0:T(8,128)S(1)}, f32[10,128]{1,0:T(8,128)S(1)}, u32[]{:S(2)}, u32[]{:S(2)}) collective-permute-start(f32[10,128]{1,0:T(8,128)S(1)} %get-tuple-element.805), channel_id=1, source_target_pairs={{0,3},{1,2},{2,1},{3,0},{4,7},{5,6},{6,5},{7,4},{8,11},{9,10},{10,... | collective-permute-start | bytes 15368 | tf_op jit(solution)/shard_map/ppermute | solution.py:290
